TPU v7x, 128 devices: a whole 4x4x4 slice. The times are simulated.
128 devices in a mesh: enc: 8 (over z, core), ctx: 16 (over y, x).
Axes of the slice: x: 4, y: 4, z: 4, core: 2. Of those that a mesh axis runs over, the one named last changes fastest.
Arguments:
- patches: bfloat16 [6144, 1280], P('enc'), may hold values from -17 to 17
- patch_image: int32 [6144], P('enc'), may hold values from 63 to 1535, as said below
- vit_gain: float32 [1280], replicated, may hold values from 0.1 to 1.9
- vit_qkv: bfloat16 [1280, 16, 240], P(None, 'ctx')
- vit_proj: bfloat16 [1280, 1280], P('ctx'), may hold values from -0.15625 to 0.15625
- merge_gain: float32 [1280], replicated, may hold values from 0.1 to 1.9
- merge_up: bfloat16 [5120, 5120], P(None, 'ctx'), may hold values from -0.078125 to 0.078125
- merge_down: bfloat16 [5120, 8192], P('ctx', 'enc'), may hold values from -0.078125 to 0.078125
- text_embed: bfloat16 [6144, 8192], P('ctx', 'enc'), may hold values from -17 to 17
- placeholder_unit: int32 [6144], replicated, may hold values from -1 to 1535, as said below
- doc_id: int32 [6144], replicated, may hold values from 0 to 31, never falling along the last dimension, each value on 1 to 3456 neighbouring positions
- dec_gain: float32 [8192], replicated, may hold values from 0.1 to 1.9
- dec_wq: bfloat16 [8192, 4096], P(None, 'enc')
- dec_wk: bfloat16 [8192, 1024], P(None, 'enc')
- dec_wv: bfloat16 [8192, 1024], P(None, 'enc'), may hold values from -0.0625 to 0.0625
Outputs:
- attended: bfloat16 [6144, 4096], P('ctx', 'enc')
Inputs may be any that keep to these rules, and one draw needn't show every extreme that they name: `patch_image`: the patches of an image are consecutive, start at a multiple of 4, number a multiple of 4 and at most 256, and lie within one aligned block of 768 patches; image numbers never fall and differ between images; in every such block some image has exactly 256 patches. `placeholder_unit`: -1 marks a text position. Every unit appears exactly once; the units of one image fill consecutive placeholders in their order; the placeholders of an aligned block of 384 positions are consecutive and number at most 192, and some block holds exactly 192. `doc_id`: document numbers never fall; a document has at most 3456 positions, and some document exactly 3456.
All inputs are finite; a program needn't handle non-finite values.
Results may differ from a plain program's by a relative error of at most 0.0085.
Values may be sent and summed in bfloat16 or wider, within the bound.
A program may use at most 128 MiB of HBM per device.

v0:
```python
import functools
import math

import jax
import jax.numpy as jnp
from jax import lax
from jax.experimental import pallas as pl
from jax.experimental.pallas import tpu as pltpu
from jax.sharding import PartitionSpec as P

MESH = pl.DeviceIdType.MESH
VMEM = pltpu.VMEM
F32 = jnp.float32
BF16 = jnp.bfloat16

HD = 128
QPK = 4
EPSILON = 1e-06
NEGATIVE = -1e30
SIDE = 4


def places():
    e, c = lax.axis_index("enc"), lax.axis_index("ctx")
    return e // 2, lax.rem(e, 2), c // SIDE, lax.rem(c, SIDE)


def at_device(z, core, y, x):
    return {"enc": z * 2 + core, "ctx": y * SIDE + x}


def ring(position, distance):
    return lax.rem(position + distance, SIDE)


def remote(source, target, send_sem, recv_sem, device):
    return pltpu.make_async_remote_copy(
        src_ref=source,
        dst_ref=target,
        send_sem=send_sem,
        recv_sem=recv_sem,
        device_id=device,
        device_id_type=MESH,
    )


def greet():
    z, core, y, x = places()
    barrier = pltpu.get_barrier_semaphore()
    peers = []
    for d in range(1, SIDE):
        peers.append(at_device(z, core, y, ring(x, d)))
        peers.append(at_device(z, core, ring(y, d), x))
        peers.append(at_device(ring(z, d), core, y, x))
    peers.append(at_device(z, 1 - core, y, x))
    for peer in peers:
        pl.semaphore_signal(barrier, inc=1, device_id=peer, device_id_type=MESH)
    pl.semaphore_wait(barrier, len(peers))


class Gather:
    def __init__(self, buf, own, cut, sems, columns=None, own_sem=None):
        self.buf, self.own, self.own_sem = buf, own, own_sem
        self.send, self.recv = sems
        cols = slice(None) if columns is None else columns
        self.part_a = (slice(0, cut), cols)
        self.part_b = (slice(cut, own.shape[0]), cols)

    def start(self, phase, pairs):
        z, core, y, x = places()
        copies = []
        for d in range(1, SIDE):
            for way, (source, target) in enumerate(pairs):
                along_x = way == phase
                device = (
                    at_device(z, core, y, ring(x, d))
                    if along_x
                    else at_device(z, core, ring(y, d), x)
                )
                sem = (2 * phase + way, d - 1)
                copies.append(
                    remote(source, target, self.send.at[sem], self.recv.at[sem], device)
                )
        for copy in copies:
            copy.start()
        return copies

    def first(self):
        z, core, y, x = places()
        if self.own_sem is not None:
            self.own_copy = pltpu.make_async_copy(self.own, self.buf.at[y, x], self.own_sem)
            self.own_copy.start()
        self.one = self.start(
            0,
            [
                (self.own.at[part], self.buf.at[(y, x) + part])
                for part in (self.part_a, self.part_b)
            ],
        )

    def second(self):
        z, core, y, x = places()
        if self.own_sem is not None:
            self.own_copy.wait()
        for copy in self.one:
            copy.wait_recv()
        rows_a = self.buf.at[(y, slice(None)) + self.part_a]
        rows_b = self.buf.at[(slice(None), x) + self.part_b]
        self.two = self.start(1, [(rows_a, rows_a), (rows_b, rows_b)])

    def finish(self):
        for copy in self.two:
            copy.wait_recv()

    def drain(self):
        for copy in self.one + self.two:
            copy.wait_send()


class EncGather:
    def __init__(self, buf, sems):
        self.buf = buf
        self.send, self.recv = sems

    def first(self, own):
        z, core, y, x = places()
        slot = z * 2 + core
        copies = [
            remote(
                own,
                self.buf.at[slot],
                self.send.at[d - 1],
                self.recv.at[d - 1],
                at_device(ring(z, d), core, y, x),
            )
            for d in range(1, SIDE)
        ]
        copies.append(
            remote(
                own,
                self.buf.at[slot],
                self.send.at[3],
                self.recv.at[3],
                at_device(z, 1 - core, y, x),
            )
        )
        for copy in copies:
            copy.start()
        self.copies = copies

    def second(self):
        z, core, y, x = places()
        self.handed = []
        for d in range(1, SIDE):
            self.copies[d - 1].wait_recv()
            slot = ring(z, SIDE - d) * 2 + core
            copy = remote(
                self.buf.at[slot],
                self.buf.at[slot],
                self.send.at[3 + d],
                self.recv.at[3 + d],
                at_device(z, 1 - core, y, x),
            )
            copy.start()
            self.handed.append(copy)

    def finish(self):
        self.copies[3].wait_recv()
        for copy in self.handed:
            copy.wait_recv()

    def drain(self):
        for copy in self.copies + self.handed:
            copy.wait_send()


def normed(wide, gain):
    center = wide - jnp.mean(wide, axis=1, keepdims=True)
    spread = jnp.mean(center * center, axis=1, keepdims=True)
    return (center * lax.rsqrt(spread + EPSILON) * gain).astype(BF16)


def gelu(x):
    return 0.5 * x * (1.0 + lax.erf(x * math.sqrt(0.5)))


def row_scale(total, count):
    return lax.rsqrt(total / count + EPSILON)


def tower_kernel(
    image_row,
    gain,
    merge_gain,
    dec_gain,
    token_code,
    placeholder,
    patches_hbm,
    qkv_hbm,
    proj_hbm,
    up_hbm,
    text_hbm,
    down_hbm,
    wq_hbm,
    wk_hbm,
    wv_hbm,
    text_q,
    text_kv,
    unit_qkv,
    unit_code,
    patches,
    qkv,
    proj,
    up,
    down,
    w_s,
    q_s,
    k_s,
    v_s,
    o_s,
    lhs_s,
    norm_s,
    heads_all,
    proj_all,
    text_a,
    text_b,
    hidden_all,
    part_a,
    part_b,
    got_a,
    got_b,
    sum_a,
    sum_b,
    got_a2,
    got_b2,
    rows_all,
    acc_s,
    kv_own_a,
    kv_own_b,
    unit_own,
    local_sem,
    proj_s,
    proj_r,
    heads_s,
    heads_r,
    swap_s,
    swap_r,
    text_as,
    text_ar,
    text_bs,
    text_br,
    hid_s,
    hid_r,
    rs_s,
    rs_r,
    row_s,
    row_r,
    kva_s,
    kva_r,
    kvb_s,
    kvb_r,
    uq_s,
    uq_r,
):
    z, core, y, x = places()
    slot = z * 2 + core
    rows, width = patches.shape
    head = proj.shape[0]
    groups = heads_all.shape[3] // head
    group_rows = rows // groups
    side_cols = pl.ds(pl.multiple_of(core * (width // 2), 128), width // 2)
    blocks, tokens, cols = text_a.shape
    model = blocks * cols
    nq, nk = wq_hbm.shape[1], wk_hbm.shape[1]
    wide = nq + 2 * nk
    own_units = unit_own.shape[0]
    half = cols // 2
    chunk = 256

    def load(index, source, target):
        copy = pltpu.make_async_copy(source, target, local_sem.at[index])
        copy.start()
        return copy

    proj_load = load(0, proj_hbm, proj)
    patches_load = load(1, patches_hbm, patches)
    qkv_load = load(2, qkv_hbm, qkv)
    text_loads = [
        load(3, text_hbm.at[0:tokens], text_a.at[slot]),
        load(4, text_hbm.at[tokens:], text_b.at[slot]),
    ]
    up_load = load(5, up_hbm, up)
    down_load = load(6, down_hbm, down)
    w_loads = [
        load(7, wq_hbm, w_s.at[:, 0:nq]),
        load(8, wk_hbm, w_s.at[:, nq : nq + nk]),
        load(9, wv_hbm, w_s.at[:, nq + nk : wide]),
    ]
    proj_load.wait()
    greet()
    proj_gather = Gather(proj_all, proj, 48, (proj_s, proj_r), columns=side_cols)
    proj_gather.first()
    text_gathers = [EncGather(text_a, (text_as, text_ar)), EncGather(text_b, (text_bs, text_br))]
    text_gathers[0].first(text_hbm.at[0:tokens])
    text_gathers[1].first(text_hbm.at[tokens:])
    proj_all[y, x, :, side_cols] = proj[:, side_cols]

    patches_load.wait()
    qkv_load.wait()

    def project(i, _):
        here = pl.ds(pl.multiple_of(i * chunk, chunk), chunk)
        block = normed(patches[here, :].astype(F32), gain[...])
        packed = lax.dot_general(
            block, qkv[...], (((1,), (1,)), ((), ())), preferred_element_type=F32
        )
        q_s[here, :] = packed[:, 0:head].astype(BF16)
        k_s[here, :] = packed[:, head : 2 * head].astype(BF16)
        v_s[here, :] = packed[:, 2 * head : 3 * head].astype(BF16)
        return 0

    lax.fori_loop(0, rows // chunk, project, 0)
    proj_gather.second()

    scaling = head ** (-0.5)

    def attend(i, _):
        here = pl.ds(pl.multiple_of(i * chunk, chunk), chunk)
        ids_col = jnp.broadcast_to(image_row[:, here], (128, chunk)).T[:, 0:1]
        scores = lax.dot_general(
            q_s[here, :], k_s[...], (((1,), (1,)), ((), ())), preferred_element_type=F32
        )
        scores = jnp.where(ids_col == image_row[...], scores * scaling, NEGATIVE)
        highest = jnp.max(scores, axis=1, keepdims=True)
        weights = jnp.exp(scores - highest)
        totals = jnp.sum(weights, axis=1, keepdims=True)
        mixture = jnp.dot(weights.astype(BF16), v_s[...], preferred_element_type=F32)
        o_s[here, :] = mixture / totals
        return 0

    lax.fori_loop(0, rows // chunk, attend, 0)
    heads_all[y, x] = jnp.concatenate(
        [o_s[j * group_rows : (j + 1) * group_rows, :] for j in range(groups)], axis=1
    ).astype(BF16)
    heads_gather = Gather(heads_all, heads_all.at[y, x], group_rows // 2, (heads_s, heads_r))
    heads_gather.first()
    proj_gather.finish()
    swap = remote(
        proj_all.at[:, :, :, side_cols],
        proj_all.at[:, :, :, side_cols],
        swap_s,
        swap_r,
        at_device(z, 1 - core, y, x),
    )
    swap.start()
    heads_gather.second()

    def scale_of(source):
        squares = jnp.zeros((source.shape[1], 128), F32)
        for b in range(blocks):
            for g in range(cols // 128):
                piece = source[b, :, g * 128 : (g + 1) * 128].astype(F32)
                squares = squares + piece * piece
        return row_scale(jnp.sum(squares, axis=1, keepdims=True), model)

    def decode(source):
        count = source.shape[1]
        scale = scale_of(source)
        acc_s[0:count, :] = jnp.zeros((count, wide), F32)

        def one_block(b, _):
            block = source[b].astype(F32) * scale * dec_gain[pl.ds(b, 1), :]
            here = pl.ds(pl.multiple_of(b * cols, cols), cols)
            acc_s[0:count, :] += jnp.dot(
                block.astype(BF16), w_s[here, :], preferred_element_type=F32
            )
            return 0

        lax.fori_loop(0, blocks, one_block, 0)

    def text_part(index, source, kv_own):
        text_loads[index].wait()
        text_gathers[index].second()
        text_gathers[index].finish()
        decode(source)
        text_q[index] = acc_s[:, 0:nq].astype(BF16)
        kv_own[...] = acc_s[:, nq:].astype(BF16)

    for w_load in w_loads:
        w_load.wait()
    text_part(0, text_a, kv_own_a)
    kv_a = Gather(
        text_kv.at[0], kv_own_a, tokens // 2, (kva_s, kva_r), own_sem=local_sem.at[10]
    )
    kv_a.first()
    swap.wait_recv()
    heads_gather.finish()

    for j in range(groups):
        lhs_s[j * group_rows : (j + 1) * group_rows, :] = jnp.concatenate(
            [
                heads_all[a, b, :, j * head : (j + 1) * head].astype(F32)
                for a in range(SIDE)
                for b in range(SIDE)
            ],
            axis=1,
        ).astype(BF16)
    kv_a.second()

    def merge(i, _):
        here = pl.ds(pl.multiple_of(i * chunk, chunk), chunk)
        terms = jnp.dot(
            lhs_s[here, :], proj_all[...].reshape(width, width), preferred_element_type=F32
        )
        out = (patches[here, :].astype(F32) + terms).astype(BF16)
        ready = normed(out.astype(F32), merge_gain[...]).astype(F32)
        for g in range(width // 128):
            norm_s[g, here, :] = ready[:, g * 128 : (g + 1) * 128]
        return 0

    lax.fori_loop(0, rows // chunk, merge, 0)
    units = rows // 4
    up_load.wait()
    total = jnp.zeros((units, up.shape[0]), F32)
    for k in range(4):
        quarter = jnp.concatenate(
            [norm_s[g, pl.ds(k, units, stride=4), :] for g in range(width // 128)], axis=1
        ).astype(BF16)
        total = total + lax.dot_general(
            quarter,
            up[:, k * width : (k + 1) * width],
            (((1,), (1,)), ((), ())),
            preferred_element_type=F32,
        )
    hidden_all[slot] = gelu(total).astype(BF16)
    hidden_gather = EncGather(hidden_all, (hid_s, hid_r))
    hidden_gather.first(hidden_all.at[slot])
    text_part(1, text_b, kv_own_b)
    kv_b = Gather(
        text_kv.at[1], kv_own_b, tokens // 2, (kvb_s, kvb_r), own_sem=local_sem.at[11]
    )
    hidden_gather.second()
    down_load.wait()
    hidden_gather.finish()

    one = []
    for d in (1, 2, 3, 0):
        xp, yp = ring(x, d), ring(y, d)
        lhs_a = jnp.concatenate(
            [
                hidden_all[
                    2 * v + xp // 2,
                    pl.ds(pl.multiple_of(lax.rem(xp, 2) * own_units, own_units), own_units),
                    :,
                ]
                for v in range(SIDE)
            ],
            axis=0,
        )
        part_a[d] = jnp.dot(lhs_a, down[:, 0:half], preferred_element_type=F32).astype(BF16)
        if d:
            copy = remote(
                part_a.at[d],
                got_a.at[d - 1],
                rs_s.at[0, d - 1],
                rs_r.at[0, d - 1],
                at_device(z, core, y, xp),
            )
            copy.start()
            one.append(copy)
        lhs_b = jnp.concatenate([hidden_all[2 * yp], hidden_all[2 * yp + 1]], axis=0)
        part_b[d] = jnp.dot(lhs_b, down[:, half:], preferred_element_type=F32).astype(BF16)
        if d:
            copy = remote(
                part_b.at[d],
                got_b.at[d - 1],
                rs_s.at[1, d - 1],
                rs_r.at[1, d - 1],
                at_device(z, core, yp, x),
            )
            copy.start()
            one.append(copy)
    kv_b.first()

    lane_unit = lax.broadcasted_iota(jnp.int32, (128, 128), 0)

    def units_block(b, _):
        unit = lane_unit + b * 128
        found = jnp.zeros((128, 128), jnp.int32)
        for r in range(placeholder.shape[0]):
            found = found + jnp.where(
                placeholder[r : r + 1, :] == unit, token_code[r : r + 1, :], 0
            )
        unit_code[pl.ds(b, 1), :] = jnp.sum(found.T, axis=0, keepdims=True)
        return 0

    lax.fori_loop(0, unit_code.shape[0], units_block, 0)

    for copy in one:
        copy.wait_recv()

    def summed(own, others):
        return sum((others[d].astype(F32) for d in range(SIDE - 1)), own.astype(F32))

    def own_rows(index):
        return pl.ds(pl.multiple_of(index * own_units, own_units), own_units)

    sum_a[...] = summed(part_a[0], got_a).astype(BF16)
    sum_b[...] = summed(part_b[0], got_b).astype(BF16)
    two = []
    for d in range(1, SIDE):
        xp, yp = ring(x, d), ring(y, d)
        two.append(
            remote(
                sum_a.at[own_rows(yp)],
                got_a2.at[d - 1],
                rs_s.at[2, d - 1],
                rs_r.at[2, d - 1],
                at_device(z, core, yp, x),
            )
        )
        two.append(
            remote(
                sum_b.at[own_rows(xp)],
                got_b2.at[d - 1],
                rs_s.at[3, d - 1],
                rs_r.at[3, d - 1],
                at_device(z, core, y, xp),
            )
        )
    for copy in two:
        copy.start()
    for copy in two:
        copy.wait_recv()
    rows_all[slot] = jnp.concatenate(
        [summed(sum_a[own_rows(y), :], got_a2), summed(sum_b[own_rows(x), :], got_b2)], axis=1
    ).astype(BF16)

    rows_gather = EncGather(rows_all, (row_s, row_r))
    rows_gather.first(rows_all.at[slot])
    kv_b.second()
    rows_gather.second()
    rows_gather.finish()
    decode(rows_all)
    unit_own[...] = acc_s[0:own_units, :].astype(BF16)
    unit_gather = Gather(
        unit_qkv, unit_own, own_units // 2, (uq_s, uq_r), own_sem=local_sem.at[12]
    )
    unit_gather.first()
    unit_gather.second()
    unit_gather.finish()
    kv_a.finish()
    kv_b.finish()
    swap.wait_send()
    for copy in one + two:
        copy.wait_send()
    for gather in [proj_gather, heads_gather, kv_a, kv_b, unit_gather]:
        gather.drain()
    for gather in text_gathers + [hidden_gather, rows_gather]:
        gather.drain()


def tower(
    image_row,
    gain,
    merge_gain,
    dec_gain,
    token_code,
    placeholder,
    patches,
    qkv,
    proj,
    up,
    text,
    down,
    wq,
    wk,
    wv,
):
    rows, width = patches.shape
    head = proj.shape[0]
    groups = 8
    units = rows // 4
    cols = text.shape[1]
    tokens = text.shape[0] // 2
    nq, nk = wq.shape[1], wk.shape[1]
    wide = nq + 2 * nk
    own_units = 8 * units // (SIDE * SIDE)
    side_units = own_units * SIDE
    half = cols // 2
    dma = pltpu.SemaphoreType.DMA
    whole = pl.BlockSpec(memory_space=VMEM)
    anywhere = pl.BlockSpec(memory_space=pl.ANY)

    def both(shape):
        return [dma(shape), dma(shape)]

    return pl.pallas_call(
        tower_kernel,
        out_shape=(
            jax.ShapeDtypeStruct((2, tokens, nq), BF16),
            jax.ShapeDtypeStruct((2, SIDE, SIDE, tokens, 2 * nk), BF16),
            jax.ShapeDtypeStruct((SIDE, SIDE, own_units, wide), BF16),
            jax.ShapeDtypeStruct((own_units * 16 // 128, 128), jnp.int32),
        ),
        in_specs=[whole] * 6 + [anywhere] * 9,
        out_specs=(whole, anywhere, anywhere, whole),
        scratch_shapes=[
            VMEM((rows, width), BF16),
            VMEM(qkv.shape, BF16),
            VMEM((head, width), BF16),
            VMEM(up.shape, BF16),
            VMEM(down.shape, BF16),
            VMEM((8 * cols, wide), BF16),
            VMEM((rows, head), BF16),
            VMEM((rows, head), BF16),
            VMEM((rows, head), BF16),
            VMEM((rows, head), F32),
            VMEM((rows, width), BF16),
            VMEM((width // 128, rows, 128), F32),
            VMEM((SIDE, SIDE, rows // groups, groups * head), BF16),
            VMEM((SIDE, SIDE, head, width), BF16),
            VMEM((8, tokens, cols), BF16),
            VMEM((8, tokens, cols), BF16),
            VMEM((8, units, up.shape[0]), BF16),
            VMEM((SIDE, side_units, half), BF16),
            VMEM((SIDE, side_units, half), BF16),
            VMEM((SIDE - 1, side_units, half), BF16),
            VMEM((SIDE - 1, side_units, half), BF16),
            VMEM((side_units, half), BF16),
            VMEM((side_units, half), BF16),
            VMEM((SIDE - 1, own_units, half), BF16),
            VMEM((SIDE - 1, own_units, half), BF16),
            VMEM((8, own_units, cols), BF16),
            VMEM((tokens, wide), F32),
            VMEM((tokens, 2 * nk), BF16),
            VMEM((tokens, 2 * nk), BF16),
            VMEM((own_units, wide), BF16),
            dma((13,)),
            *both((4, 3)),
            *both((4, 3)),
            *both(()),
            *both((7,)),
            *both((7,)),
            *both((7,)),
            *both((4, 3)),
            *both((7,)),
            *both((4, 3)),
            *both((4, 3)),
            *both((4, 3)),
        ],
        compiler_params=pltpu.CompilerParams(
            collective_id=1, has_side_effects=True, vmem_limit_bytes=60 * 2**20
        ),
        name="tower",
    )(
        image_row,
        gain,
        merge_gain,
        dec_gain,
        token_code,
        placeholder,
        patches,
        qkv,
        proj,
        up,
        text,
        down,
        wq,
        wk,
        wv,
    )


def attention_kernel(
    where_ref,
    doc_smem,
    text_q,
    unit_code,
    doc_rows,
    unit_rows,
    text_kv_hbm,
    unit_qkv_hbm,
    out,
    text_kv,
    unit_qkv,
    load_sem,
    q_s,
    peak_s,
    total_s,
    mix_s,
    bias_s,
):
    tokens, nq = text_q.shape
    nk = text_kv.shape[2] // 2
    unit_load = pltpu.make_async_copy(unit_qkv_hbm, unit_qkv, load_sem.at[0])
    unit_load.start()
    text_loads = []
    for p in range(2):
        here = slice(p * (tokens // 2), (p + 1) * (tokens // 2))
        text_loads.append(
            pltpu.make_async_copy(text_kv_hbm.at[p], text_kv.at[:, here, :], load_sem.at[1 + p])
        )
        text_loads[p].start()
    heads = nq // HD
    units = unit_qkv.shape[0] * unit_qkv.shape[1]
    mine = where_ref[0]
    first_doc = doc_smem[mine, 0]
    scale = HD ** (-0.5) * math.log2(math.e)

    def column(rows):
        return jnp.concatenate(
            [jnp.broadcast_to(rows[g : g + 1, :], (128, 128)).T for g in range(tokens // 128)],
            axis=0,
        )

    query_doc = column(doc_rows[mine])
    query_unit = column(unit_rows[mine])
    query_at = mine * tokens + lax.broadcasted_iota(jnp.int32, (tokens, 128), 0)
    lane = lax.broadcasted_iota(jnp.int32, (tokens, 128), 1)

    picked = jnp.zeros((tokens, nq), F32)
    chunk = 384
    unit_load.wait()
    per_chunk = chunk // unit_qkv.shape[1]
    for b in range(units // chunk):
        chosen = jnp.concatenate(
            [
                (query_unit == lane + (b * chunk + g * 128)).astype(F32)
                for g in range(chunk // 128)
            ],
            axis=1,
        ).astype(BF16)
        source = unit_qkv[b * per_chunk : (b + 1) * per_chunk, :, 0:nq].reshape(chunk, nq)
        picked = picked + jnp.dot(chosen, source, preferred_element_type=F32)
    for j in range(heads):
        part = slice(j * HD, (j + 1) * HD)
        q_s[j] = jnp.where(query_unit >= 0, picked[:, part], text_q[:, part].astype(F32)).astype(
            BF16
        )
    peak_s[...] = jnp.full_like(peak_s, NEGATIVE)
    total_s[...] = jnp.zeros_like(total_s)
    mix_s[...] = jnp.zeros_like(mix_s)

    def fold(keys, values):
        for j in range(heads):
            scores = lax.dot_general(
                q_s[j], keys, (((1,), (1,)), ((), ())), preferred_element_type=F32
            )
            scores = scores + bias_s[...]
            before = peak_s[j]
            peak = jnp.maximum(before, jnp.max(scores, axis=1, keepdims=True))
            factor = jnp.exp2((before - peak) * scale)
            wide_peak = jnp.concatenate([peak] * (scores.shape[1] // 128), axis=1)
            weights = jnp.exp2((scores - wide_peak) * scale)
            peak_s[j] = peak
            total_s[j] = total_s[j] * factor + jnp.sum(weights, axis=1, keepdims=True)
            mix_s[j] = mix_s[j] * factor + jnp.dot(
                weights.astype(BF16), values, preferred_element_type=F32
            )

    def text_block(s, _):
        docs, unit_of = doc_rows[s], unit_rows[s]
        for g in range(tokens // 128):
            part = slice(g * 128, (g + 1) * 128)
            key_at = s * tokens + g * 128 + lane
            same = query_doc == docs[g : g + 1, :]
            text = unit_of[g : g + 1, :] < 0
            allowed = same & (key_at <= query_at) & text
            bias_s[:, part] = jnp.where(allowed, 0.0, NEGATIVE)
        block = text_kv[s]
        fold(block[:, 0:nk], block[:, nk:])
        return 0

    begin = jnp.int32(0)
    for s in range(doc_smem.shape[0]):
        begin = begin + (doc_smem[s, tokens - 1] < first_doc).astype(jnp.int32)
    for text_load in text_loads:
        text_load.wait()
    lax.fori_loop(begin, mine + 1, text_block, 0)

    def unit_block(b, _):
        for g in range(chunk // 128):
            code = unit_code[pl.ds(b * (chunk // 128) + g, 1), :]
            allowed = (query_doc == (code & 63)) & ((code >> 6) <= query_at)
            bias_s[:, g * 128 : (g + 1) * 128] = jnp.where(allowed, 0.0, NEGATIVE)
        block = unit_qkv[pl.ds(b * per_chunk, per_chunk), :, nq:].reshape(chunk, 2 * nk)
        fold(block[:, 0:nk], block[:, nk:])
        return 0

    lax.fori_loop(0, units // chunk, unit_block, 0)
    for j in range(heads):
        out[:, j * HD : (j + 1) * HD] = (mix_s[j] / total_s[j]).astype(BF16)


def attention(where, doc, text_q, text_kv, unit_qkv, unit_code, placeholder):
    tokens, nq = text_q.shape
    heads = nq // HD
    shards = text_kv.shape[1]
    whole = pl.BlockSpec(memory_space=VMEM)
    anywhere = pl.BlockSpec(memory_space=pl.ANY)
    scalars = pl.BlockSpec(memory_space=pltpu.SMEM)
    return pl.pallas_call(
        attention_kernel,
        out_shape=jax.ShapeDtypeStruct((tokens, nq), BF16),
        in_specs=[scalars, scalars] + [whole] * 4 + [anywhere] * 2,
        out_specs=whole,
        scratch_shapes=[
            VMEM((shards, tokens, text_kv.shape[3]), BF16),
            VMEM(unit_qkv.shape, BF16),
            pltpu.SemaphoreType.DMA((3,)),
            VMEM((heads, tokens, HD), BF16),
            VMEM((heads, tokens, 128), F32),
            VMEM((heads, tokens, 128), F32),
            VMEM((heads, tokens, HD), F32),
            VMEM((tokens, tokens), F32),
        ],
        compiler_params=pltpu.CompilerParams(vmem_limit_bytes=60 * 2**20),
        name="attention",
    )(
        where,
        doc,
        text_q,
        unit_code,
        doc.reshape(-1, tokens // 128, 128),
        placeholder.reshape(-1, tokens // 128, 128),
        text_kv,
        unit_qkv,
    )


def body(
    patches,
    patch_image,
    vit_gain,
    vit_qkv,
    vit_proj,
    merge_gain,
    merge_up,
    merge_down,
    text_embed,
    placeholder_unit,
    doc_id,
    dec_gain,
    dec_wq,
    dec_wk,
    dec_wv,
):
    tokens = text_embed.shape[0]
    token_code = jnp.arange(doc_id.shape[0], dtype=jnp.int32) * 64 + doc_id
    text_q, text_kv, unit_qkv, unit_code = tower(
        patch_image.reshape(1, -1),
        vit_gain.reshape(1, -1),
        merge_gain.reshape(1, -1),
        dec_gain.reshape(8, -1),
        token_code.reshape(-1, 128),
        placeholder_unit.reshape(-1, 128),
        patches,
        vit_qkv.transpose(1, 2, 0).reshape(-1, vit_qkv.shape[0]),
        vit_proj,
        merge_up.T,
        text_embed,
        merge_down,
        dec_wq,
        dec_wk,
        dec_wv,
    )
    where = lax.axis_index("ctx").astype(jnp.int32).reshape(1)
    return attention(
        where,
        doc_id.reshape(-1, tokens),
        text_q.reshape(tokens, -1),
        text_kv.reshape(2, 16, tokens // 2, -1),
        unit_qkv.reshape(16, -1, unit_qkv.shape[-1]),
        unit_code,
        placeholder_unit.reshape(-1, tokens),
    )


def solution(mesh):
    placed = (
        P("enc", None),
        P("enc"),
        P(),
        P(None, "ctx", None),
        P("ctx", None),
        P(),
        P(None, "ctx"),
        P("ctx", "enc"),
        P("ctx", "enc"),
        P(),
        P(),
        P(),
        P(None, "enc"),
        P(None, "enc"),
        P(None, "enc"),
    )
    return jax.shard_map(
        body, mesh=mesh, in_specs=placed, out_specs=P("ctx", "enc"), check_vma=False
    )
```

profile of v0, /device:TPU:16, one launch (start us, length us, event | category | flops | bytes accessed | tf_op | source)
XLA Modules:
  0.0 158.7 jit_solution(17737610785948750645)
XLA Ops:
  0.0 1.3 reshape.38.image_row
  1.3 1.3 reshape.39.gain
  2.6 1.3 reshape.40.merge_gain
  3.9 1.4 reshape.37.doc_smem
  5.2 1.4 add_bitcast_fusion.token_code
  6.6 1.4 reshape.41.dec_gain
  8.0 1.4 reshape_reshape.7.unit_rows
  9.3 1.4 reshape_reshape.6.doc_rows
  10.7 125.3 %tower.1 = (bf16[2,192,512]{2,1,0:T(8,128)(2,1)}, bf16[2,4,4,192,256]{4,3,2,1,0:T(8,128)(2,1)}, bf16[4,4,96,768]{3,2,1,0:T(8,128)(2,1)}, s32[12,128]{1,0:T(8,128)}) custom-call(s32[1,768]{1,0:T(1,128)} %reshape.38.image_row, f32[1,1280]{1,0:T(1,128)} %reshape.39.gain, f32[1,1280]{1,0:T(1,128)} %reshape.40.merge_gain, f32[8,1024]{1,0:T(8,128)} %reshape.41.dec_gain, ...), custom_call_target="tpu_custom_call" | custom-call | tf_op jit(solution)/shard_map/tower/pallas_call | solution.py:598
  136.0 22.5 %attention.1 = bf16[384,512]{1,0:T(8,128)(2,1)} custom-call(s32[1]{0:T(128)} %bitcast.where_ref, s32[16,384]{1,0:T(8,128)} %reshape.37.doc_smem, bf16[384,512]{1,0:T(8,128)(2,1)} %bitcast.15, s32[12,128]{1,0:T(8,128)} %get-tuple-element.10.unit_code, s32[16,3,128]{2,1,0:T(4,128)} %reshape_reshape.6.doc_rows, s32[16,3,128]{2,1,0:T(4,128)} %reshape_reshape.7.unit_rows, ...), custom_call_target="tpu_custom_call" | custom-call | tf_op jit(solution)/shard_map/attention/pallas_call | solution.py:803
where the time goes:
time: 161 us; the launch traced here: 159 us
  Pallas kernels  148 us (92%)
  local copies, waits for them, and re-layouts  9.32 us (6%)
    pallas_call x1, Pallas kernels, tower(): pl.pallas_call(tower_kernel, out_shape=(jax.ShapeDtypeStruct((2, tokens,...  125 us
    pallas_call x1, Pallas kernels, attention(): pl.pallas_call(attention_kernel, out_shape=jax.ShapeDtypeStruct((tokens,...  22.5 us

commit v1 on v0

v1 whole, which is shorter than its diff:
```python
import functools
import math

import jax
import jax.numpy as jnp
from jax import lax
from jax.experimental import pallas as pl
from jax.experimental.pallas import tpu as pltpu
from jax.sharding import PartitionSpec as P

MESH = pl.DeviceIdType.MESH
VMEM = pltpu.VMEM
F32 = jnp.float32
BF16 = jnp.bfloat16

HD = 128
QPK = 4
EPSILON = 1e-06
NEGATIVE = -1e30
SIDE = 4


def places():
    e, c = lax.axis_index("enc"), lax.axis_index("ctx")
    return e // 2, lax.rem(e, 2), c // SIDE, lax.rem(c, SIDE)


def at_device(z, core, y, x):
    return {"enc": z * 2 + core, "ctx": y * SIDE + x}


def ring(position, distance):
    return lax.rem(position + distance, SIDE)


def remote(source, target, send_sem, recv_sem, device):
    return pltpu.make_async_remote_copy(
        src_ref=source,
        dst_ref=target,
        send_sem=send_sem,
        recv_sem=recv_sem,
        device_id=device,
        device_id_type=MESH,
    )


def ring_peers():
    z, core, y, x = places()
    peers = []
    for d in range(1, SIDE):
        peers.append(at_device(z, core, y, ring(x, d)))
        peers.append(at_device(z, core, ring(y, d), x))
        peers.append(at_device(ring(z, d), core, y, x))
    peers.append(at_device(z, 1 - core, y, x))
    return peers


def greet():
    for peer in ring_peers():
        pl.semaphore_signal(
            pltpu.get_barrier_semaphore(), inc=1, device_id=peer, device_id_type=MESH
        )


def meet():
    pl.semaphore_wait(pltpu.get_barrier_semaphore(), len(ring_peers()))


def row_of(ref, first, count):
    return jnp.concatenate([ref[pl.ds(first + g, 1), :] for g in range(count)], axis=1)


def column_of(ref, first, count):
    return jnp.concatenate(
        [jnp.broadcast_to(ref[pl.ds(first + g, 1), :], (128, 128)).T for g in range(count)],
        axis=0,
    )


class Gather:
    def __init__(self, buf, own, parts, sems, own_sem=None):
        self.buf, self.own, self.own_sem = buf, own, own_sem
        self.send, self.recv = sems
        self.part_a, self.part_b = parts

    def start(self, phase, pairs):
        z, core, y, x = places()
        copies = []
        for d in range(1, SIDE):
            for way, (source, target) in enumerate(pairs):
                along_x = way == phase
                device = (
                    at_device(z, core, y, ring(x, d))
                    if along_x
                    else at_device(z, core, ring(y, d), x)
                )
                sem = (2 * phase + way, d - 1)
                copies.append(
                    remote(source, target, self.send.at[sem], self.recv.at[sem], device)
                )
        for copy in copies:
            copy.start()
        return copies

    def first(self):
        z, core, y, x = places()
        if self.own_sem is not None:
            self.own_copy = pltpu.make_async_copy(self.own, self.buf.at[y, x], self.own_sem)
            self.own_copy.start()
        self.one = self.start(
            0,
            [
                (self.own.at[part], self.buf.at[(y, x) + part])
                for part in (self.part_a, self.part_b)
            ],
        )

    def second(self):
        z, core, y, x = places()
        if self.own_sem is not None:
            self.own_copy.wait()
        for copy in self.one:
            copy.wait_recv()
        rows_a = self.buf.at[(y, slice(None)) + self.part_a]
        rows_b = self.buf.at[(slice(None), x) + self.part_b]
        self.two = self.start(1, [(rows_a, rows_a), (rows_b, rows_b)])

    def finish(self):
        for copy in self.two:
            copy.wait_recv()

    def drain(self):
        for copy in self.one + self.two:
            copy.wait_send()


class EncGather:
    def __init__(self, buf, sems):
        self.buf = buf
        self.send, self.recv = sems

    def first(self, own):
        z, core, y, x = places()
        slot = z * 2 + core
        copies = [
            remote(
                own,
                self.buf.at[slot],
                self.send.at[d - 1],
                self.recv.at[d - 1],
                at_device(ring(z, d), core, y, x),
            )
            for d in range(1, SIDE)
        ]
        copies.append(
            remote(
                own,
                self.buf.at[slot],
                self.send.at[3],
                self.recv.at[3],
                at_device(z, 1 - core, y, x),
            )
        )
        for copy in copies:
            copy.start()
        self.copies = copies

    def second(self):
        z, core, y, x = places()
        self.handed = []
        for d in range(1, SIDE):
            self.copies[d - 1].wait_recv()
            slot = ring(z, SIDE - d) * 2 + core
            copy = remote(
                self.buf.at[slot],
                self.buf.at[slot],
                self.send.at[3 + d],
                self.recv.at[3 + d],
                at_device(z, 1 - core, y, x),
            )
            copy.start()
            self.handed.append(copy)

    def finish(self):
        self.copies[3].wait_recv()
        for copy in self.handed:
            copy.wait_recv()

    def drain(self):
        for copy in self.copies + self.handed:
            copy.wait_send()


class RelayGather:
    def __init__(self, buf, sems):
        self.buf = buf
        self.send, self.recv = sems

    def copy(self, index, source, target, device):
        copy = remote(source, target, self.send.at[index], self.recv.at[index], device)
        copy.start()
        self.copies.append(copy)

    def first(self, own):
        z, core, y, x = places()
        self.copies = []
        here = self.buf.at[z * 2 + core]
        self.copy(0, own, here, at_device(ring(z, 1), core, y, x))
        self.copy(1, own, here, at_device(ring(z, 3), core, y, x))
        self.copy(2, own, here, at_device(z, 1 - core, y, x))

    def relay(self):
        z, core, y, x = places()
        middle = self.buf.shape[1] // 2
        left, right = ring(z, 3) * 2 + core, ring(z, 1) * 2 + core
        self.copies[0].wait_recv()
        low = self.buf.at[left, 0:middle]
        self.copy(3, low, low, at_device(ring(z, 1), core, y, x))
        self.copies[1].wait_recv()
        high = self.buf.at[right, middle:]
        self.copy(4, high, high, at_device(ring(z, 3), core, y, x))
        for index, block in ((5, left), (6, right)):
            whole = self.buf.at[block]
            self.copy(index, whole, whole, at_device(z, 1 - core, y, x))

    def second(self):
        z, core, y, x = places()
        self.copies[3].wait_recv()
        self.copies[4].wait_recv()
        far = self.buf.at[ring(z, 2) * 2 + core]
        self.copy(7, far, far, at_device(z, 1 - core, y, x))

    def finish(self):
        for index in (2, 5, 6, 7):
            self.copies[index].wait_recv()

    def drain(self):
        for copy in self.copies:
            copy.wait_send()


def halves(rows):
    return (slice(0, rows // 2), slice(None)), (slice(rows // 2, rows), slice(None))


def normed(wide, gain):
    center = wide - jnp.mean(wide, axis=1, keepdims=True)
    spread = jnp.mean(center * center, axis=1, keepdims=True)
    return (center * lax.rsqrt(spread + EPSILON) * gain).astype(BF16)


def gelu(x):
    return 0.5 * x * (1.0 + lax.erf(x * math.sqrt(0.5)))


def row_scale(total, count):
    return lax.rsqrt(total / count + EPSILON)


def tower_kernel(
    image,
    gain_rows,
    merge_gain_rows,
    dec_gain,
    doc,
    placeholder,
    patches_hbm,
    qkv_hbm,
    proj_hbm,
    up_hbm,
    text_hbm,
    down_hbm,
    wq_hbm,
    wk_hbm,
    wv_hbm,
    text_q,
    text_kv,
    unit_qkv,
    unit_code,
    patches,
    qkv,
    proj,
    up,
    down,
    w_s,
    q_s,
    k_s,
    v_s,
    o_s,
    lhs_s,
    norm_s,
    heads_all,
    proj_all,
    text_a,
    text_b,
    hidden_all,
    part_a,
    part_b,
    got_a,
    got_b,
    sum_a,
    sum_b,
    got_a2,
    got_b2,
    rows_all,
    acc_s,
    kv_own_a,
    kv_own_b,
    unit_own,
    code_s,
    local_sem,
    proj_s,
    proj_r,
    heads_s,
    heads_r,
    swap_s,
    swap_r,
    text_as,
    text_ar,
    text_bs,
    text_br,
    hid_s,
    hid_r,
    rs_s,
    rs_r,
    row_s,
    row_r,
    kva_s,
    kva_r,
    kvb_s,
    kvb_r,
    uq_s,
    uq_r,
):
    z, core, y, x = places()
    slot = z * 2 + core
    rows, width = patches.shape
    head = proj.shape[0]
    groups = heads_all.shape[3] // head
    group_rows = rows // groups
    side_cols = pl.ds(pl.multiple_of(core * (width // 2), 128), width // 2)
    blocks, tokens, cols = text_a.shape
    model = blocks * cols
    nq, nk = wq_hbm.shape[1], wk_hbm.shape[1]
    wide = nq + 2 * nk
    own_units = 2 * unit_own.shape[1]
    half = cols // 2
    chunk = 256

    def load(index, source, target):
        copy = pltpu.make_async_copy(source, target, local_sem.at[index])
        copy.start()
        return copy

    patches_load = load(1, patches_hbm, patches)
    qkv_load = load(2, qkv_hbm, qkv)
    proj_load = load(0, proj_hbm, proj)
    greet()
    text_loads = [
        load(3, text_hbm.at[0:tokens], text_a.at[slot]),
        load(4, text_hbm.at[tokens:], text_b.at[slot]),
    ]
    w_loads = [
        load(7, wq_hbm, w_s.at[:, 0:nq]),
        load(8, wk_hbm, w_s.at[:, nq : nq + nk]),
        load(9, wv_hbm, w_s.at[:, nq + nk : wide]),
    ]
    up_load = load(5, up_hbm, up)
    down_load = load(6, down_hbm, down)

    gain = row_of(gain_rows, 0, width // 128)
    merge_gain = row_of(merge_gain_rows, 0, width // 128)
    image_row = row_of(image, 0, rows // 128)
    patches_load.wait()
    qkv_load.wait()

    def project(i, _):
        here = pl.ds(pl.multiple_of(i * chunk, chunk), chunk)
        block = normed(patches[here, :].astype(F32), gain)
        packed = lax.dot_general(
            block, qkv[...], (((1,), (1,)), ((), ())), preferred_element_type=F32
        )
        q_s[here, :] = packed[:, 0:head].astype(BF16)
        k_s[here, :] = packed[:, head : 2 * head].astype(BF16)
        v_s[here, :] = packed[:, 2 * head : 3 * head].astype(BF16)
        return 0

    lax.fori_loop(0, rows // chunk, project, 0)

    scaling = head ** (-0.5)

    def attend(i, _):
        here = pl.ds(pl.multiple_of(i * chunk, chunk), chunk)
        ids_col = column_of(image, i * (chunk // 128), chunk // 128)[:, 0:1]
        scores = lax.dot_general(
            q_s[here, :], k_s[...], (((1,), (1,)), ((), ())), preferred_element_type=F32
        )
        scores = jnp.where(ids_col == image_row, scores * scaling, NEGATIVE)
        highest = jnp.max(scores, axis=1, keepdims=True)
        weights = jnp.exp(scores - highest)
        totals = jnp.sum(weights, axis=1, keepdims=True)
        mixture = jnp.dot(weights.astype(BF16), v_s[...], preferred_element_type=F32)
        o_s[here, :] = mixture / totals
        return 0

    lax.fori_loop(0, rows // chunk, attend, 0)
    heads_all[y, x] = jnp.concatenate(
        [o_s[j * group_rows : (j + 1) * group_rows, :] for j in range(groups)], axis=1
    ).astype(BF16)
    proj_load.wait()
    proj_all[y, x, :, side_cols] = proj[:, side_cols]
    meet()
    proj_gather = Gather(
        proj_all,
        proj,
        ((slice(0, 48), side_cols), (slice(48, head), side_cols)),
        (proj_s, proj_r),
    )
    proj_gather.first()
    heads_gather = Gather(
        heads_all, heads_all.at[y, x], halves(group_rows), (heads_s, heads_r)
    )
    heads_gather.first()
    text_gathers = [
        RelayGather(text_a, (text_as, text_ar)),
        RelayGather(text_b, (text_bs, text_br)),
    ]
    text_gathers[0].first(text_hbm.at[0:tokens])

    def scale_of(source):
        squares = jnp.zeros((source.shape[1], 128), F32)
        for b in range(blocks):
            for g in range(cols // 128):
                piece = source[b, :, g * 128 : (g + 1) * 128].astype(F32)
                squares = squares + piece * piece
        return row_scale(jnp.sum(squares, axis=1, keepdims=True), model)

    def decode(source):
        count = source.shape[1]
        scale = scale_of(source)
        acc_s[0:count, :] = jnp.zeros((count, wide), F32)

        def one_block(b, _):
            block = source[b].astype(F32) * scale * row_of(dec_gain, b * (cols // 128), cols // 128)
            here = pl.ds(pl.multiple_of(b * cols, cols), cols)
            acc_s[0:count, :] += jnp.dot(
                block.astype(BF16), w_s[here, :], preferred_element_type=F32
            )
            return 0

        lax.fori_loop(0, blocks, one_block, 0)

    def text_part(index, source, kv_own):
        text_loads[index].wait()
        text_gathers[index].finish()
        decode(source)
        text_q[index] = acc_s[:, 0:nq].astype(BF16)
        kv_own[...] = acc_s[:, nq:].astype(BF16)

    proj_gather.second()
    heads_gather.second()
    text_gathers[0].relay()
    text_gathers[1].first(text_hbm.at[tokens:])
    proj_gather.finish()
    swap = remote(
        proj_all.at[:, :, :, side_cols],
        proj_all.at[:, :, :, side_cols],
        swap_s,
        swap_r,
        at_device(z, 1 - core, y, x),
    )
    swap.start()
    for w_load in w_loads:
        w_load.wait()
    text_gathers[0].second()
    text_part(0, text_a, kv_own_a)
    kv_a = Gather(
        text_kv.at[0], kv_own_a, halves(tokens), (kva_s, kva_r), own_sem=local_sem.at[10]
    )
    kv_a.first()
    text_gathers[1].relay()
    swap.wait_recv()
    heads_gather.finish()

    for j in range(groups):
        lhs_s[j * group_rows : (j + 1) * group_rows, :] = jnp.concatenate(
            [
                heads_all[a, b, :, j * head : (j + 1) * head].astype(F32)
                for a in range(SIDE)
                for b in range(SIDE)
            ],
            axis=1,
        ).astype(BF16)

    def merge(i, _):
        here = pl.ds(pl.multiple_of(i * chunk, chunk), chunk)
        terms = jnp.dot(
            lhs_s[here, :], proj_all[...].reshape(width, width), preferred_element_type=F32
        )
        out = (patches[here, :].astype(F32) + terms).astype(BF16)
        ready = normed(out.astype(F32), merge_gain).astype(F32)
        for g in range(width // 128):
            norm_s[g, here, :] = ready[:, g * 128 : (g + 1) * 128]
        return 0

    lax.fori_loop(0, rows // chunk, merge, 0)
    kv_a.second()
    text_gathers[1].second()
    units = rows // 4
    up_load.wait()
    total = jnp.zeros((units, up.shape[0]), F32)
    for k in range(4):
        quarter = jnp.concatenate(
            [norm_s[g, pl.ds(k, units, stride=4), :] for g in range(width // 128)], axis=1
        ).astype(BF16)
        total = total + lax.dot_general(
            quarter,
            up[:, k * width : (k + 1) * width],
            (((1,), (1,)), ((), ())),
            preferred_element_type=F32,
        )
    hidden = gelu(total).astype(BF16)
    share = own_units // 2
    hidden_gathers = []
    for h in range(2):
        hidden_all[h, slot] = jnp.concatenate(
            [
                hidden[(2 * v + h) * share : (2 * v + h + 1) * share, :]
                for v in range(units // own_units)
            ],
            axis=0,
        )
        hidden_gathers.append(EncGather(hidden_all.at[h], (hid_s.at[h], hid_r.at[h])))
        hidden_gathers[h].first(hidden_all.at[h, slot])
    text_part(1, text_b, kv_own_b)
    kv_b = Gather(
        text_kv.at[1], kv_own_b, halves(tokens), (kvb_s, kvb_r), own_sem=local_sem.at[11]
    )
    kv_b.first()
    down_load.wait()

    lane_unit = lax.broadcasted_iota(jnp.int32, (128, 128), 0)
    position = lax.broadcasted_iota(jnp.int32, doc.shape, 0) * 128 + lax.broadcasted_iota(
        jnp.int32, doc.shape, 1
    )
    code_s[...] = position * 64 + doc[...]

    def units_block(b, _):
        unit = lane_unit + b * 128
        found = jnp.zeros((128, 128), jnp.int32)
        for r in range(placeholder.shape[0]):
            found = found + jnp.where(
                placeholder[r : r + 1, :] == unit, code_s[r : r + 1, :], 0
            )
        unit_code[pl.ds(b, 1), :] = jnp.sum(found.T, axis=0, keepdims=True)
        return 0

    one, two = [[], []], [[], []]

    def share_rows(index):
        return pl.ds(pl.multiple_of(index * share, share), share)

    def summed(own, others):
        return sum((others[d].astype(F32) for d in range(SIDE - 1)), own.astype(F32))

    def terms(h, distances):
        for d in distances:
            xp, yp = ring(x, d), ring(y, d)
            lhs_a = jnp.concatenate(
                [
                    hidden_all[h, 2 * v + xp // 2, share_rows(lax.rem(xp, 2)), :]
                    for v in range(SIDE)
                ],
                axis=0,
            )
            lhs_b = jnp.concatenate(
                [
                    hidden_all[h, 2 * yp + v // 2, share_rows(v % 2), :]
                    for v in range(SIDE)
                ],
                axis=0,
            )
            for way, (lhs, columns, part, got, device) in enumerate(
                (
                    (lhs_a, slice(0, half), part_a, got_a, at_device(z, core, y, xp)),
                    (lhs_b, slice(half, cols), part_b, got_b, at_device(z, core, yp, x)),
                )
            ):
                part[h, d] = jnp.dot(
                    lhs, down[:, columns], preferred_element_type=F32
                ).astype(BF16)
                if d:
                    copy = remote(
                        part.at[h, d],
                        got.at[h, d - 1],
                        rs_s.at[h, way, d - 1],
                        rs_r.at[h, way, d - 1],
                        device,
                    )
                    copy.start()
                    one[h].append(copy)

    def ring_sums(h):
        for copy in one[h]:
            copy.wait_recv()
        sum_a[h] = summed(part_a[h, 0], got_a.at[h]).astype(BF16)
        sum_b[h] = summed(part_b[h, 0], got_b.at[h]).astype(BF16)
        for d in range(1, SIDE):
            xp, yp = ring(x, d), ring(y, d)
            for way, (total_s, place, got, device) in enumerate(
                (
                    (sum_a, yp, got_a2, at_device(z, core, yp, x)),
                    (sum_b, xp, got_b2, at_device(z, core, y, xp)),
                )
            ):
                copy = remote(
                    total_s.at[h, share_rows(place)],
                    got.at[h, d - 1],
                    rs_s.at[h, 2 + way, d - 1],
                    rs_r.at[h, 2 + way, d - 1],
                    device,
                )
                copy.start()
                two[h].append(copy)

    rows_gathers = [
        EncGather(rows_all.at[h], (row_s.at[h], row_r.at[h])) for h in range(2)
    ]

    def full_sums(h):
        for copy in two[h]:
            copy.wait_recv()
        rows_all[h, slot] = jnp.concatenate(
            [
                summed(sum_a[h, share_rows(y), :], got_a2.at[h]),
                summed(sum_b[h, share_rows(x), :], got_b2.at[h]),
            ],
            axis=1,
        ).astype(BF16)
        rows_gathers[h].first(rows_all.at[h, slot])

    unit_parts = (
        (slice(0, share), slice(0, wide // 2)),
        (slice(0, share), slice(wide // 2, wide)),
    )
    unit_gathers = [
        Gather(
            unit_qkv.at[h],
            unit_own.at[h],
            unit_parts,
            (uq_s.at[h], uq_r.at[h]),
            own_sem=local_sem.at[12 + h],
        )
        for h in range(2)
    ]

    def decode_units(h):
        decode(rows_all.at[h])
        unit_own[h] = acc_s[0:share, :].astype(BF16)
        unit_gathers[h].first()

    hidden_gathers[0].second()
    hidden_gathers[0].finish()
    terms(0, (2, 1, 3, 0))
    hidden_gathers[1].second()
    hidden_gathers[1].finish()
    terms(1, (2,))
    lax.fori_loop(0, unit_code.shape[0], units_block, 0)
    ring_sums(0)
    terms(1, (1, 3, 0))
    full_sums(0)
    ring_sums(1)
    kv_b.second()
    rows_gathers[0].second()
    full_sums(1)
    rows_gathers[0].finish()
    decode_units(0)
    rows_gathers[1].second()
    unit_gathers[0].second()
    rows_gathers[1].finish()
    decode_units(1)
    unit_gathers[1].second()
    for gather in unit_gathers + [kv_a, kv_b]:
        gather.finish()
    swap.wait_send()
    for copy in one[0] + one[1] + two[0] + two[1]:
        copy.wait_send()
    for gather in [proj_gather, heads_gather, kv_a, kv_b] + unit_gathers:
        gather.drain()
    for gather in text_gathers + hidden_gathers + rows_gathers:
        gather.drain()


def tower(
    image,
    gain,
    merge_gain,
    dec_gain,
    doc,
    placeholder,
    patches,
    qkv,
    proj,
    up,
    text,
    down,
    wq,
    wk,
    wv,
):
    rows, width = patches.shape
    head = proj.shape[0]
    groups = 8
    units = rows // 4
    cols = text.shape[1]
    tokens = text.shape[0] // 2
    nq, nk = wq.shape[1], wk.shape[1]
    wide = nq + 2 * nk
    own_units = 8 * units // (SIDE * SIDE)
    share = own_units // 2
    half = cols // 2
    dma = pltpu.SemaphoreType.DMA
    whole = pl.BlockSpec(memory_space=VMEM)
    anywhere = pl.BlockSpec(memory_space=pl.ANY)

    def both(shape):
        return [dma(shape), dma(shape)]

    return pl.pallas_call(
        tower_kernel,
        out_shape=(
            jax.ShapeDtypeStruct((2, tokens, nq), BF16),
            jax.ShapeDtypeStruct((2, SIDE, SIDE, tokens, 2 * nk), BF16),
            jax.ShapeDtypeStruct((2, SIDE, SIDE, share, wide), BF16),
            jax.ShapeDtypeStruct((own_units * 16 // 128, 128), jnp.int32),
        ),
        in_specs=[whole] * 6 + [anywhere] * 9,
        out_specs=(whole, anywhere, anywhere, whole),
        scratch_shapes=[
            VMEM((rows, width), BF16),
            VMEM(qkv.shape, BF16),
            VMEM((head, width), BF16),
            VMEM(up.shape, BF16),
            VMEM(down.shape, BF16),
            VMEM((8 * cols, wide), BF16),
            VMEM((rows, head), BF16),
            VMEM((rows, head), BF16),
            VMEM((rows, head), BF16),
            VMEM((rows, head), F32),
            VMEM((rows, width), BF16),
            VMEM((width // 128, rows, 128), F32),
            VMEM((SIDE, SIDE, rows // groups, groups * head), BF16),
            VMEM((SIDE, SIDE, head, width), BF16),
            VMEM((8, tokens, cols), BF16),
            VMEM((8, tokens, cols), BF16),
            VMEM((2, 8, units // 2, up.shape[0]), BF16),
            VMEM((2, SIDE, SIDE * share, half), BF16),
            VMEM((2, SIDE, SIDE * share, half), BF16),
            VMEM((2, SIDE - 1, SIDE * share, half), BF16),
            VMEM((2, SIDE - 1, SIDE * share, half), BF16),
            VMEM((2, SIDE * share, half), BF16),
            VMEM((2, SIDE * share, half), BF16),
            VMEM((2, SIDE - 1, share, half), BF16),
            VMEM((2, SIDE - 1, share, half), BF16),
            VMEM((2, 8, share, cols), BF16),
            VMEM((tokens, wide), F32),
            VMEM((tokens, 2 * nk), BF16),
            VMEM((tokens, 2 * nk), BF16),
            VMEM((2, share, wide), BF16),
            VMEM(doc.shape, jnp.int32),
            dma((14,)),
            *both((4, 3)),
            *both((4, 3)),
            *both(()),
            *both((8,)),
            *both((8,)),
            *both((2, 7)),
            *both((2, 4, 3)),
            *both((2, 7)),
            *both((4, 3)),
            *both((4, 3)),
            *both((2, 4, 3)),
        ],
        compiler_params=pltpu.CompilerParams(
            collective_id=1, has_side_effects=True, vmem_limit_bytes=60 * 2**20
        ),
        name="tower",
    )(
        image,
        gain,
        merge_gain,
        dec_gain,
        doc,
        placeholder,
        patches,
        qkv,
        proj,
        up,
        text,
        down,
        wq,
        wk,
        wv,
    )


def attention_kernel(
    where_ref,
    doc_smem,
    text_q,
    unit_code,
    doc_rows,
    unit_rows,
    text_kv_hbm,
    unit_qkv_hbm,
    out,
    text_kv,
    unit_qkv,
    load_sem,
    q_s,
    peak_s,
    mix_s,
    bias_s,
):
    tokens, nq = text_q.shape
    nk = text_kv.shape[2] // 2
    unit_loads = []
    for p in range(2):
        share = unit_qkv.shape[1] // 2
        here = slice(p * share, (p + 1) * share)
        unit_loads.append(
            pltpu.make_async_copy(
                unit_qkv_hbm.at[p], unit_qkv.at[:, here, :], load_sem.at[2 + p]
            )
        )
        unit_loads[p].start()
    text_loads = []
    for p in range(2):
        here = slice(p * (tokens // 2), (p + 1) * (tokens // 2))
        text_loads.append(
            pltpu.make_async_copy(text_kv_hbm.at[p], text_kv.at[:, here, :], load_sem.at[p])
        )
        text_loads[p].start()
    heads = nq // HD
    units = unit_qkv.shape[0] * unit_qkv.shape[1]
    mine = where_ref[0]
    first_doc = doc_smem[mine * tokens]
    scale = HD ** (-0.5) * math.log2(math.e)

    lines = tokens // 128
    query_doc = column_of(doc_rows, mine * lines, lines)
    query_unit = column_of(unit_rows, mine * lines, lines)
    query_at = mine * tokens + lax.broadcasted_iota(jnp.int32, (tokens, 128), 0)
    lane = lax.broadcasted_iota(jnp.int32, (tokens, 128), 1)

    picked = jnp.zeros((tokens, nq), F32)
    chunk = 384
    for unit_load in unit_loads:
        unit_load.wait()
    per_chunk = chunk // unit_qkv.shape[1]
    for b in range(units // chunk):
        chosen = jnp.concatenate(
            [
                (query_unit == lane + (b * chunk + g * 128)).astype(F32)
                for g in range(chunk // 128)
            ],
            axis=1,
        ).astype(BF16)
        source = unit_qkv[b * per_chunk : (b + 1) * per_chunk, :, 0:nq].reshape(chunk, nq)
        picked = picked + jnp.dot(chosen, source, preferred_element_type=F32)
    for j in range(heads):
        part = slice(j * HD, (j + 1) * HD)
        q_s[j] = jnp.where(query_unit >= 0, picked[:, part], text_q[:, part].astype(F32)).astype(
            BF16
        )
    peak_s[...] = jnp.full_like(peak_s, NEGATIVE)
    mix_s[...] = jnp.zeros_like(mix_s)
    row_chunk = 128

    def fold(keys, values):
        values = jnp.concatenate([values, jnp.ones_like(values)], axis=1)
        for r in range(0, tokens, row_chunk):
            here = slice(r, r + row_chunk)
            for j in range(heads):
                scores = lax.dot_general(
                    q_s[j, here, :], keys, (((1,), (1,)), ((), ())), preferred_element_type=F32
                )
                scores = scores + bias_s[here, :]
                before = peak_s[j, here, :]
                peak = jnp.maximum(before, jnp.max(scores, axis=1, keepdims=True))
                factor = jnp.exp2((before - peak) * scale)
                wide_peak = jnp.concatenate([peak] * (scores.shape[1] // 128), axis=1)
                weights = jnp.exp2((scores - wide_peak) * scale).astype(BF16)
                peak_s[j, here, :] = peak
                mix_s[j, here, :] = mix_s[j, here, :] * jnp.concatenate(
                    [factor] * 2, axis=1
                ) + jnp.dot(weights, values, preferred_element_type=F32)

    def text_block(i, _):
        blocks = []
        for t in range(2):
            s = begin + 2 * i + t
            held = jnp.minimum(s, text_kv.shape[0] - 1)
            for g in range(lines):
                key_at = s * tokens + g * 128 + lane
                same = query_doc == doc_rows[pl.ds(held * lines + g, 1), :]
                text = unit_rows[pl.ds(held * lines + g, 1), :] < 0
                allowed = same & (key_at <= query_at) & text
                bias_s[:, t * tokens + g * 128 : t * tokens + (g + 1) * 128] = jnp.where(
                    allowed, 0.0, NEGATIVE
                )
            blocks.append(text_kv[held])
        both = jnp.concatenate(blocks, axis=0)
        fold(both[:, 0:nk], both[:, nk:])
        return 0

    begin = jnp.int32(0)
    for s in range(text_kv.shape[0]):
        begin = begin + (doc_smem[(s + 1) * tokens - 1] < first_doc).astype(jnp.int32)
    for text_load in text_loads:
        text_load.wait()
    lax.fori_loop(0, (mine + 2 - begin) // 2, text_block, 0)

    pair = 2 * chunk

    def unit_block(b, _):
        for g in range(pair // 128):
            code = unit_code[pl.ds(b * (pair // 128) + g, 1), :]
            allowed = (query_doc == (code & 63)) & ((code >> 6) <= query_at)
            bias_s[:, g * 128 : (g + 1) * 128] = jnp.where(allowed, 0.0, NEGATIVE)
        block = unit_qkv[pl.ds(b * 2 * per_chunk, 2 * per_chunk), :, nq:].reshape(pair, 2 * nk)
        fold(block[:, 0:nk], block[:, nk:])
        return 0

    lax.fori_loop(0, units // pair, unit_block, 0)
    for j in range(heads):
        out[:, j * HD : (j + 1) * HD] = (mix_s[j, :, 0:HD] / mix_s[j, :, HD:]).astype(BF16)


def attention(where, doc, text_q, text_kv, unit_qkv, unit_code, placeholder):
    tokens, nq = text_q.shape
    heads = nq // HD
    shards = text_kv.shape[1]
    whole = pl.BlockSpec(memory_space=VMEM)
    anywhere = pl.BlockSpec(memory_space=pl.ANY)
    scalars = pl.BlockSpec(memory_space=pltpu.SMEM)
    return pl.pallas_call(
        attention_kernel,
        out_shape=jax.ShapeDtypeStruct((tokens, nq), BF16),
        in_specs=[scalars, scalars] + [whole] * 4 + [anywhere] * 2,
        out_specs=whole,
        scratch_shapes=[
            VMEM((shards, tokens, text_kv.shape[3]), BF16),
            VMEM((shards, 2 * unit_qkv.shape[2], unit_qkv.shape[3]), BF16),
            pltpu.SemaphoreType.DMA((4,)),
            VMEM((heads, tokens, HD), BF16),
            VMEM((heads, tokens, 128), F32),
            VMEM((heads, tokens, 2 * HD), F32),
            VMEM((tokens, 2 * tokens), F32),
        ],
        compiler_params=pltpu.CompilerParams(vmem_limit_bytes=60 * 2**20),
        name="attention",
    )(
        where,
        doc,
        text_q,
        unit_code,
        doc.reshape(-1, 128),
        placeholder.reshape(-1, 128),
        text_kv,
        unit_qkv,
    )


def body(
    patches,
    patch_image,
    vit_gain,
    vit_qkv,
    vit_proj,
    merge_gain,
    merge_up,
    merge_down,
    text_embed,
    placeholder_unit,
    doc_id,
    dec_gain,
    dec_wq,
    dec_wk,
    dec_wv,
):
    tokens = text_embed.shape[0]
    text_q, text_kv, unit_qkv, unit_code = tower(
        patch_image.reshape(-1, 128),
        vit_gain.reshape(-1, 128),
        merge_gain.reshape(-1, 128),
        dec_gain.reshape(-1, 128),
        doc_id.reshape(-1, 128),
        placeholder_unit.reshape(-1, 128),
        patches,
        vit_qkv.transpose(1, 2, 0).reshape(-1, vit_qkv.shape[0]),
        vit_proj,
        merge_up.T,
        text_embed,
        merge_down,
        dec_wq,
        dec_wk,
        dec_wv,
    )
    where = lax.axis_index("ctx").astype(jnp.int32).reshape(1)
    return attention(
        where,
        doc_id,
        text_q.reshape(tokens, -1),
        text_kv.reshape(2, 16, tokens // 2, -1),
        unit_qkv.reshape(2, 16, -1, unit_qkv.shape[-1]),
        unit_code,
        placeholder_unit,
    )


def solution(mesh):
    placed = (
        P("enc", None),
        P("enc"),
        P(),
        P(None, "ctx", None),
        P("ctx", None),
        P(),
        P(None, "ctx"),
        P("ctx", "enc"),
        P("ctx", "enc"),
        P(),
        P(),
        P(),
        P(None, "enc"),
        P(None, "enc"),
        P(None, "enc"),
    )
    return jax.shard_map(
        body, mesh=mesh, in_specs=placed, out_specs=P("ctx", "enc"), check_vma=False
    )
```

time: 161 us -> 131 us (0.81)
  the two profiles are of different devices: /device:TPU:16 before, /device:TPU:23 now
where the time goes in v1:
time: 131 us; the launch traced here: 130 us
  Pallas kernels  130 us (99%)
    pallas_call x1, Pallas kernels, tower(): pl.pallas_call(tower_kernel, out_shape=(jax.ShapeDtypeStruct((2, tokens,...  112 us
    pallas_call x1, Pallas kernels, attention(): pl.pallas_call(attention_kernel, out_shape=jax.ShapeDtypeStruct((tokens,...  18.3 us

profile of v1, /device:TPU:23, one launch (start us, length us, event | category | flops | bytes accessed | tf_op | source)
XLA Modules:
  0.0 130.3 jit_solution(18017288434817243471)
XLA Ops:
  0.0 111.8 %tower.1 = (bf16[2,192,512]{2,1,0:T(8,128)(2,1)}, bf16[2,4,4,192,256]{4,3,2,1,0:T(8,128)(2,1)}, bf16[2,4,4,48,768]{4,3,2,1,0:T(8,128)(2,1)}, s32[12,128]{1,0:T(8,128)}) custom-call(s32[6,128]{1,0:T(8,128)} %bitcast.26, f32[10,128]{1,0:T(8,128)} %bitcast.24, f32[10,128]{1,0:T(8,128)} %bitcast.25, f32[64,128]{1,0:T(8,128)} %bitcast.23, s32[48,128]{1,0:T(8,128)} %bitcast.19, ...), custom_call_target="tpu_custom_call" | custom-call | tf_op jit(solution)/shard_map/tower/pallas_call | solution.py:729
  111.8 18.3 %attention.1 = bf16[384,512]{1,0:T(8,128)(2,1)} custom-call(s32[1]{0:T(128)} %bitcast.where_ref, s32[6144]{0:T(1024)} %doc_smem.1, bf16[384,512]{1,0:T(8,128)(2,1)} %bitcast.18, s32[12,128]{1,0:T(8,128)} %get-tuple-element.10.unit_code, s32[48,128]{1,0:T(8,128)} %bitcast.20, s32[48,128]{1,0:T(8,128)} %bitcast.22, bf16[2,16,192,256]{3,2,1,0:T(8,128)(2,1)} %bitcast.15, ...), custom_call_target="tpu_custom_call" | custom-call | tf_op jit(solution)/shard_map/attention/pallas_call | solution.py:947

commit v2 on v1

--- a/solution.py
+++ b/solution.py
@@ -83,10 +83,10 @@
         self.send, self.recv = sems
         self.part_a, self.part_b = parts
 
-    def start(self, phase, pairs):
+    def start(self, phase, pairs, distances):
         z, core, y, x = places()
-        copies = []
-        for d in range(1, SIDE):
+        copies = {}
+        for d in distances:
             for way, (source, target) in enumerate(pairs):
                 along_x = way == phase
                 device = (
@@ -95,10 +95,10 @@
                     else at_device(z, core, ring(y, d), x)
                 )
                 sem = (2 * phase + way, d - 1)
-                copies.append(
-                    remote(source, target, self.send.at[sem], self.recv.at[sem], device)
+                copies[way, d] = remote(
+                    source, target, self.send.at[sem], self.recv.at[sem], device
                 )
-        for copy in copies:
+        for copy in copies.values():
             copy.start()
         return copies
 
@@ -113,25 +113,52 @@
                 (self.own.at[part], self.buf.at[(y, x) + part])
                 for part in (self.part_a, self.part_b)
             ],
-        )
-
-    def second(self):
+            (1, 2, 3),
+        )
+
+    def lines(self, row, column, some=slice(None)):
+        return (
+            self.buf.at[(row, some) + self.part_a],
+            self.buf.at[(some, column) + self.part_b],
+        )
+
+    def second(self, relayed=False):
         z, core, y, x = places()
         if self.own_sem is not None:
             self.own_copy.wait()
-        for copy in self.one:
+        for copy in self.one.values():
             copy.wait_recv()
-        rows_a = self.buf.at[(y, slice(None)) + self.part_a]
-        rows_b = self.buf.at[(slice(None), x) + self.part_b]
-        self.two = self.start(1, [(rows_a, rows_a), (rows_b, rows_b)])
+        self.relayed = relayed
+        self.two = self.start(
+            1, [(line, line) for line in self.lines(y, x)], (1, 3) if relayed else (1, 2, 3)
+        )
+        self.handed = {}
+
+    def relay(self):
+        z, core, y, x = places()
+        for index, (d, some) in enumerate(((1, slice(0, 2)), (3, slice(2, 4)))):
+            for way in range(2):
+                self.two[way, d].wait_recv()
+                line = self.lines(ring(y, SIDE - d), ring(x, SIDE - d), some)[way]
+                device = (
+                    at_device(z, core, ring(y, d), x)
+                    if way == 0
+                    else at_device(z, core, y, ring(x, d))
+                )
+                sem = (2 + way, 1 + 2 * index)
+                self.handed[way, d] = remote(
+                    line, line, self.send.at[sem], self.recv.at[sem], device
+                )
+                self.handed[way, d].start()
 
     def finish(self):
-        for copy in self.two:
+        for copy in (self.handed if self.relayed else self.two).values():
             copy.wait_recv()
 
     def drain(self):
-        for copy in self.one + self.two:
-            copy.wait_send()
+        for copies in (self.one, self.two, self.handed):
+            for copy in copies.values():
+                copy.wait_send()
 
 
 class EncGather:
@@ -195,19 +222,27 @@
     def __init__(self, buf, sems):
         self.buf = buf
         self.send, self.recv = sems
+        self.copies = {}
 
     def copy(self, index, source, target, device):
         copy = remote(source, target, self.send.at[index], self.recv.at[index], device)
         copy.start()
-        self.copies.append(copy)
-
-    def first(self, own):
+        self.copies[index] = copy
+
+    def first(self, own, high):
         z, core, y, x = places()
-        self.copies = []
-        here = self.buf.at[z * 2 + core]
-        self.copy(0, own, here, at_device(ring(z, 1), core, y, x))
-        self.copy(1, own, here, at_device(ring(z, 3), core, y, x))
-        self.copy(2, own, here, at_device(z, 1 - core, y, x))
+        middle, rows = self.buf.shape[1] // 2, self.buf.shape[1]
+        slot = z * 2 + core
+        part = slice(middle, rows) if high else slice(0, middle)
+        for index, d in ((8, 1), (9, 3)) if high else ((0, 1), (1, 3)):
+            self.copy(
+                index,
+                own.at[part],
+                self.buf.at[slot, part],
+                at_device(ring(z, d), core, y, x),
+            )
+        if not high:
+            self.copy(2, own, self.buf.at[slot], at_device(z, 1 - core, y, x))
 
     def relay(self):
         z, core, y, x = places()
@@ -216,9 +251,11 @@
         self.copies[0].wait_recv()
         low = self.buf.at[left, 0:middle]
         self.copy(3, low, low, at_device(ring(z, 1), core, y, x))
-        self.copies[1].wait_recv()
+        self.copies[9].wait_recv()
         high = self.buf.at[right, middle:]
         self.copy(4, high, high, at_device(ring(z, 3), core, y, x))
+        self.copies[1].wait_recv()
+        self.copies[8].wait_recv()
         for index, block in ((5, left), (6, right)):
             whole = self.buf.at[block]
             self.copy(index, whole, whole, at_device(z, 1 - core, y, x))
@@ -235,7 +272,7 @@
             self.copies[index].wait_recv()
 
     def drain(self):
-        for copy in self.copies:
+        for copy in self.copies.values():
             copy.wait_send()
 
 
@@ -298,6 +335,8 @@
     part_b,
     got_a,
     got_b,
+    both_a,
+    both_b,
     sum_a,
     sum_b,
     got_a2,
@@ -387,26 +426,6 @@
 
     lax.fori_loop(0, rows // chunk, project, 0)
 
-    scaling = head ** (-0.5)
-
-    def attend(i, _):
-        here = pl.ds(pl.multiple_of(i * chunk, chunk), chunk)
-        ids_col = column_of(image, i * (chunk // 128), chunk // 128)[:, 0:1]
-        scores = lax.dot_general(
-            q_s[here, :], k_s[...], (((1,), (1,)), ((), ())), preferred_element_type=F32
-        )
-        scores = jnp.where(ids_col == image_row, scores * scaling, NEGATIVE)
-        highest = jnp.max(scores, axis=1, keepdims=True)
-        weights = jnp.exp(scores - highest)
-        totals = jnp.sum(weights, axis=1, keepdims=True)
-        mixture = jnp.dot(weights.astype(BF16), v_s[...], preferred_element_type=F32)
-        o_s[here, :] = mixture / totals
-        return 0
-
-    lax.fori_loop(0, rows // chunk, attend, 0)
-    heads_all[y, x] = jnp.concatenate(
-        [o_s[j * group_rows : (j + 1) * group_rows, :] for j in range(groups)], axis=1
-    ).astype(BF16)
     proj_load.wait()
     proj_all[y, x, :, side_cols] = proj[:, side_cols]
     meet()
@@ -417,15 +436,38 @@
         (proj_s, proj_r),
     )
     proj_gather.first()
-    heads_gather = Gather(
-        heads_all, heads_all.at[y, x], halves(group_rows), (heads_s, heads_r)
-    )
-    heads_gather.first()
     text_gathers = [
         RelayGather(text_a, (text_as, text_ar)),
         RelayGather(text_b, (text_bs, text_br)),
     ]
-    text_gathers[0].first(text_hbm.at[0:tokens])
+    text_gathers[0].first(text_hbm.at[0:tokens], False)
+    text_gathers[0].first(text_hbm.at[0:tokens], True)
+    text_gathers[1].first(text_hbm.at[tokens:], False)
+
+    scaling = head ** (-0.5)
+
+    def attend(i, _):
+        here = pl.ds(pl.multiple_of(i * chunk, chunk), chunk)
+        ids_col = column_of(image, i * (chunk // 128), chunk // 128)[:, 0:1]
+        scores = lax.dot_general(
+            q_s[here, :], k_s[...], (((1,), (1,)), ((), ())), preferred_element_type=F32
+        )
+        scores = jnp.where(ids_col == image_row, scores * scaling, NEGATIVE)
+        highest = jnp.max(scores, axis=1, keepdims=True)
+        weights = jnp.exp(scores - highest)
+        totals = jnp.sum(weights, axis=1, keepdims=True)
+        mixture = jnp.dot(weights.astype(BF16), v_s[...], preferred_element_type=F32)
+        o_s[here, :] = mixture / totals
+        return 0
+
+    lax.fori_loop(0, rows // chunk, attend, 0)
+    heads_all[y, x] = jnp.concatenate(
+        [o_s[j * group_rows : (j + 1) * group_rows, :] for j in range(groups)], axis=1
+    ).astype(BF16)
+    heads_gather = Gather(
+        heads_all, heads_all.at[y, x], halves(group_rows), (heads_s, heads_r)
+    )
+    heads_gather.first()
 
     def scale_of(source):
         squares = jnp.zeros((source.shape[1], 128), F32)
@@ -457,10 +499,31 @@
         text_q[index] = acc_s[:, 0:nq].astype(BF16)
         kv_own[...] = acc_s[:, nq:].astype(BF16)
 
-    proj_gather.second()
-    heads_gather.second()
+    lane_unit = lax.broadcasted_iota(jnp.int32, (128, 128), 0)
+    position = lax.broadcasted_iota(jnp.int32, doc.shape, 0) * 128 + lax.broadcasted_iota(
+        jnp.int32, doc.shape, 1
+    )
+    code_s[...] = position * 64 + doc[...]
+
+    def units_block(b, _):
+        unit = lane_unit + b * 128
+        found = jnp.zeros((128, 128), jnp.int32)
+        for r in range(placeholder.shape[0]):
+            found = found + jnp.where(
+                placeholder[r : r + 1, :] == unit, code_s[r : r + 1, :], 0
+            )
+        unit_code[pl.ds(b, 1), :] = jnp.sum(found.T, axis=0, keepdims=True)
+        return 0
+
+    proj_gather.second(relayed=True)
+    heads_gather.second(relayed=True)
     text_gathers[0].relay()
-    text_gathers[1].first(text_hbm.at[tokens:])
+    text_gathers[1].first(text_hbm.at[tokens:], True)
+    lax.fori_loop(0, unit_code.shape[0] // 2, units_block, 0)
+    proj_gather.relay()
+    lax.fori_loop(unit_code.shape[0] // 2, unit_code.shape[0], units_block, 0)
+    heads_gather.relay()
+    text_gathers[0].second()
     proj_gather.finish()
     swap = remote(
         proj_all.at[:, :, :, side_cols],
@@ -472,7 +535,6 @@
     swap.start()
     for w_load in w_loads:
         w_load.wait()
-    text_gathers[0].second()
     text_part(0, text_a, kv_own_a)
     kv_a = Gather(
         text_kv.at[0], kv_own_a, halves(tokens), (kva_s, kva_r), own_sem=local_sem.at[10]
@@ -504,7 +566,7 @@
         return 0
 
     lax.fori_loop(0, rows // chunk, merge, 0)
-    kv_a.second()
+    kv_a.second(relayed=True)
     text_gathers[1].second()
     units = rows // 4
     up_load.wait()
@@ -536,26 +598,11 @@
     kv_b = Gather(
         text_kv.at[1], kv_own_b, halves(tokens), (kvb_s, kvb_r), own_sem=local_sem.at[11]
     )
+    kv_a.relay()
     kv_b.first()
     down_load.wait()
 
-    lane_unit = lax.broadcasted_iota(jnp.int32, (128, 128), 0)
-    position = lax.broadcasted_iota(jnp.int32, doc.shape, 0) * 128 + lax.broadcasted_iota(
-        jnp.int32, doc.shape, 1
-    )
-    code_s[...] = position * 64 + doc[...]
-
-    def units_block(b, _):
-        unit = lane_unit + b * 128
-        found = jnp.zeros((128, 128), jnp.int32)
-        for r in range(placeholder.shape[0]):
-            found = found + jnp.where(
-                placeholder[r : r + 1, :] == unit, code_s[r : r + 1, :], 0
-            )
-        unit_code[pl.ds(b, 1), :] = jnp.sum(found.T, axis=0, keepdims=True)
-        return 0
-
-    one, two = [[], []], [[], []]
+    one, two = [{}, {}], [[], []]
 
     def share_rows(index):
         return pl.ds(pl.multiple_of(index * share, share), share)
@@ -563,8 +610,28 @@
     def summed(own, others):
         return sum((others[d].astype(F32) for d in range(SIDE - 1)), own.astype(F32))
 
-    def terms(h, distances):
-        for d in distances:
+    ring_ways = (
+        (part_a, got_a, both_a, slice(0, half)),
+        (part_b, got_b, both_b, slice(half, cols)),
+    )
+    low, high = slice(0, half // 2), slice(half // 2, half)
+
+    def neighbour(way, d):
+        return at_device(z, core, y, ring(x, d)) if way == 0 else at_device(z, core, ring(y, d), x)
+
+    def pass_on(h, way, index, source, d):
+        copy = remote(
+            source,
+            ring_ways[way][1].at[h, index],
+            rs_s.at[h, way, index],
+            rs_r.at[h, way, index],
+            neighbour(way, d),
+        )
+        copy.start()
+        one[h][way, index] = copy
+
+    def terms(h):
+        for d in (2, 1, 3, 0):
             xp, yp = ring(x, d), ring(y, d)
             lhs_a = jnp.concatenate(
                 [
@@ -574,37 +641,48 @@
                 axis=0,
             )
             lhs_b = jnp.concatenate(
-                [
-                    hidden_all[h, 2 * yp + v // 2, share_rows(v % 2), :]
-                    for v in range(SIDE)
-                ],
+                [hidden_all[h, 2 * yp + v // 2, share_rows(v % 2), :] for v in range(SIDE)],
                 axis=0,
             )
-            for way, (lhs, columns, part, got, device) in enumerate(
-                (
-                    (lhs_a, slice(0, half), part_a, got_a, at_device(z, core, y, xp)),
-                    (lhs_b, slice(half, cols), part_b, got_b, at_device(z, core, yp, x)),
-                )
-            ):
+            for way, lhs in enumerate((lhs_a, lhs_b)):
+                part, got, both, columns = ring_ways[way]
                 part[h, d] = jnp.dot(
                     lhs, down[:, columns], preferred_element_type=F32
                 ).astype(BF16)
-                if d:
-                    copy = remote(
-                        part.at[h, d],
-                        got.at[h, d - 1],
-                        rs_s.at[h, way, d - 1],
-                        rs_r.at[h, way, d - 1],
-                        device,
-                    )
-                    copy.start()
-                    one[h].append(copy)
+                if d == 2:
+                    pass_on(h, way, 0, part.at[h, d, :, low], 1)
+                    pass_on(h, way, 1, part.at[h, d, :, high], 3)
+                elif d == 1:
+                    pass_on(h, way, 2, part.at[h, d, :, high], 1)
+                elif d == 3:
+                    pass_on(h, way, 3, part.at[h, d, :, low], 3)
+
+    def combine(h):
+        for way in range(2):
+            part, got, both, columns = ring_ways[way]
+            for index, (d, side) in enumerate(((1, low), (3, high))):
+                one[h][way, index].wait_recv()
+                both[h, index] = (
+                    part[h, d, :, side].astype(F32) + got[h, index].astype(F32)
+                ).astype(BF16)
+                pass_on(h, way, 4 + index, both.at[h, index], d)
+
+    def ring_total(h, way):
+        part, got, both, columns = ring_ways[way]
+        for index in range(2, 6):
+            one[h][way, index].wait_recv()
+        others = jnp.concatenate(
+            [
+                got[h, 4].astype(F32) + got[h, 3].astype(F32),
+                got[h, 2].astype(F32) + got[h, 5].astype(F32),
+            ],
+            axis=1,
+        )
+        return (part[h, 0].astype(F32) + others).astype(BF16)
 
     def ring_sums(h):
-        for copy in one[h]:
-            copy.wait_recv()
-        sum_a[h] = summed(part_a[h, 0], got_a.at[h]).astype(BF16)
-        sum_b[h] = summed(part_b[h, 0], got_b.at[h]).astype(BF16)
+        sum_a[h] = ring_total(h, 0)
+        sum_b[h] = ring_total(h, 1)
         for d in range(1, SIDE):
             xp, yp = ring(x, d), ring(y, d)
             for way, (total_s, place, got, device) in enumerate(
@@ -661,29 +739,31 @@
 
     hidden_gathers[0].second()
     hidden_gathers[0].finish()
-    terms(0, (2, 1, 3, 0))
+    terms(0)
     hidden_gathers[1].second()
     hidden_gathers[1].finish()
-    terms(1, (2,))
-    lax.fori_loop(0, unit_code.shape[0], units_block, 0)
+    combine(0)
+    terms(1)
     ring_sums(0)
-    terms(1, (1, 3, 0))
+    combine(1)
     full_sums(0)
     ring_sums(1)
-    kv_b.second()
+    kv_b.second(relayed=True)
     rows_gathers[0].second()
     full_sums(1)
     rows_gathers[0].finish()
     decode_units(0)
+    kv_b.relay()
     rows_gathers[1].second()
-    unit_gathers[0].second()
     rows_gathers[1].finish()
     decode_units(1)
+    unit_gathers[0].second(relayed=True)
     unit_gathers[1].second()
+    unit_gathers[0].relay()
     for gather in unit_gathers + [kv_a, kv_b]:
         gather.finish()
     swap.wait_send()
-    for copy in one[0] + one[1] + two[0] + two[1]:
+    for copy in [*one[0].values(), *one[1].values(), *two[0], *two[1]]:
         copy.wait_send()
     for gather in [proj_gather, heads_gather, kv_a, kv_b] + unit_gathers:
         gather.drain()
@@ -756,8 +836,10 @@
             VMEM((2, 8, units // 2, up.shape[0]), BF16),
             VMEM((2, SIDE, SIDE * share, half), BF16),
             VMEM((2, SIDE, SIDE * share, half), BF16),
-            VMEM((2, SIDE - 1, SIDE * share, half), BF16),
-            VMEM((2, SIDE - 1, SIDE * share, half), BF16),
+            VMEM((2, 6, SIDE * share, half // 2), BF16),
+            VMEM((2, 6, SIDE * share, half // 2), BF16),
+            VMEM((2, 2, SIDE * share, half // 2), BF16),
+            VMEM((2, 2, SIDE * share, half // 2), BF16),
             VMEM((2, SIDE * share, half), BF16),
             VMEM((2, SIDE * share, half), BF16),
             VMEM((2, SIDE - 1, share, half), BF16),
@@ -769,17 +851,17 @@
             VMEM((2, share, wide), BF16),
             VMEM(doc.shape, jnp.int32),
             dma((14,)),
-            *both((4, 3)),
-            *both((4, 3)),
+            *both((4, 4)),
+            *both((4, 4)),
             *both(()),
-            *both((8,)),
-            *both((8,)),
+            *both((10,)),
+            *both((10,)),
             *both((2, 7)),
-            *both((2, 4, 3)),
+            *both((2, 4, 6)),
             *both((2, 7)),
-            *both((4, 3)),
-            *both((4, 3)),
-            *both((2, 4, 3)),
+            *both((4, 4)),
+            *both((4, 4)),
+            *both((2, 4, 4)),
         ],
         compiler_params=pltpu.CompilerParams(
             collective_id=1, has_side_effects=True, vmem_limit_bytes=60 * 2**20

time: 131 us -> 122 us (0.931)
  the two profiles are of different devices: /device:TPU:23 before, /device:TPU:16 now
where the time goes in v2:
time: 122 us
  Pallas kernels  121 us (99%)
    pallas_call x1, Pallas kernels, tower(): pl.pallas_call(tower_kernel, out_shape=(jax.ShapeDtypeStruct((2, tokens,...  103 us
    pallas_call x1, Pallas kernels, attention(): pl.pallas_call(attention_kernel, out_shape=jax.ShapeDtypeStruct((tokens,...  18.3 us

profile of v2, /device:TPU:16, one launch (start us, length us, event | category | flops | bytes accessed | tf_op | source)
XLA Modules:
  0.0 121.6 jit_solution(16639539214212933688)
XLA Ops:
  0.0 103.1 %tower.1 = (bf16[2,192,512]{2,1,0:T(8,128)(2,1)}, bf16[2,4,4,192,256]{4,3,2,1,0:T(8,128)(2,1)}, bf16[2,4,4,48,768]{4,3,2,1,0:T(8,128)(2,1)}, s32[12,128]{1,0:T(8,128)}) custom-call(s32[6,128]{1,0:T(8,128)} %bitcast.26, f32[10,128]{1,0:T(8,128)} %bitcast.24, f32[10,128]{1,0:T(8,128)} %bitcast.25, f32[64,128]{1,0:T(8,128)} %bitcast.23, s32[48,128]{1,0:T(8,128)} %bitcast.19, ...), custom_call_target="tpu_custom_call" | custom-call | tf_op jit(solution)/shard_map/tower/pallas_call | solution.py:809
  103.1 18.3 %attention.1 = bf16[384,512]{1,0:T(8,128)(2,1)} custom-call(s32[1]{0:T(128)} %bitcast.where_ref, s32[6144]{0:T(1024)} %doc_smem.1, bf16[384,512]{1,0:T(8,128)(2,1)} %bitcast.18, s32[12,128]{1,0:T(8,128)} %get-tuple-element.10.unit_code, s32[48,128]{1,0:T(8,128)} %bitcast.20, s32[48,128]{1,0:T(8,128)} %bitcast.22, bf16[2,16,192,256]{3,2,1,0:T(8,128)(2,1)} %bitcast.15, ...), custom_call_target="tpu_custom_call" | custom-call | tf_op jit(solution)/shard_map/attention/pallas_call | solution.py:1029
